TPU v7x, 32 devices: a whole 2x2x4 slice. The times are simulated.
32 devices in a mesh: rows: 8 (over y, x, core), grp: 4 (over z).
Axes of the slice: x: 2, y: 2, z: 4, core: 2. Of those that a mesh axis runs over, the one named last changes fastest.
Arguments:
- pivot_columns: bfloat16 [32, 10240, 256], P('rows', 'grp'), may hold values from -6 to 6
- previous: bfloat16 [32, 10240, 512], P('rows', 'grp'), may hold values from -0.59765625 to 0.59765625
- pivots: int32 [256], replicated, may hold values from 0 to 327679, as said below
- pivot_inverse: bfloat16 [256, 256], replicated, may hold values from -0.4 to 1.5
- orbitals: bfloat16 [10240, 1024], P('grp'), may hold values from -0.0625 to 0.0625
- slab_orbitals: bfloat16 [32, 1024], replicated, may hold values from -1 to 1
Outputs:
- new_vectors: bfloat16 [32, 10240, 256], P('rows', 'grp')
- mo_block: bfloat16 [256, 1024, 1024], P('rows', None, 'grp')
Inputs may be any that keep to these rules, and one draw needn't show every extreme that they name: `pivots`: distinct entries.
All inputs are finite; a program needn't handle non-finite values.
Results may differ from a plain program's by a relative error of at most 0.0038.
The roundings to bfloat16 on the way count: a program that leaves them out, or rounds other values in their place, can miss the bound.
Values may be sent and summed in bfloat16 or wider, within the bound.
A program may use at most 128 MiB of HBM per device.

v0:
```python
import jax
import jax.numpy as jnp
from jax import lax
from jax.sharding import PartitionSpec as P

NBAS = 10240


def per_device(pivot_columns, previous, pivots, pivot_inverse, orbitals, slab_orbitals):
    mu_dev, nu_dev, prev_count = previous.shape
    pivot_count = pivot_columns.shape[2]
    row_index = lax.axis_index("rows")
    grp_index = lax.axis_index("grp")
    first_local = pivots // NBAS - row_index * mu_dev
    second_local = pivots % NBAS - grp_index * nu_dev
    owned = (
        (first_local >= 0) & (first_local < mu_dev) & (second_local >= 0) & (second_local < nu_dev)
    )
    local_row = jnp.where(owned, first_local * nu_dev + second_local, 0)
    flat_prev = previous.reshape(mu_dev * nu_dev, prev_count)
    picked = jnp.where(
        owned[:, None], jnp.take(flat_prev, local_row, axis=0).astype(jnp.float32), 0.0
    )
    pivot_rows = lax.psum(picked, ("rows", "grp")).astype(jnp.bfloat16)
    correction = jnp.dot(flat_prev, pivot_rows.T, preferred_element_type=jnp.float32)
    flat_columns = pivot_columns.reshape(mu_dev * nu_dev, pivot_count)
    residual_columns = (flat_columns.astype(jnp.float32) - correction).astype(jnp.bfloat16)
    upper = jnp.triu(pivot_inverse)
    new_flat = jnp.dot(residual_columns, upper, preferred_element_type=jnp.float32).astype(
        jnp.bfloat16
    )
    new_vectors = new_flat.reshape(mu_dev, nu_dev, pivot_count)
    half = lax.psum_scatter(
        jnp.einsum("nj,mnp->jmp", orbitals, new_vectors, preferred_element_type=jnp.float32),
        "grp",
        scatter_dimension=0,
        tiled=True,
    ).astype(jnp.bfloat16)
    summed = jnp.einsum(
        "mi,jmp->pij",
        slab_orbitals,
        lax.all_to_all(half, "rows", split_axis=2, concat_axis=1, tiled=True),
        preferred_element_type=jnp.float32,
    )
    mo_block = summed.astype(jnp.bfloat16)
    return (new_vectors, mo_block)


def solution(mesh):
    in_specs = (P("rows", "grp", None), P("rows", "grp", None), P(), P(), P("grp", None), P())
    out_specs = (P("rows", "grp", None), P("rows", None, "grp"))
    return jax.shard_map(
        per_device, mesh=mesh, in_specs=in_specs, out_specs=out_specs, check_vma=False
    )
```

profile of v0, /device:TPU:0, one launch (start us, length us, event | category | flops | bytes accessed | tf_op | source)
XLA Modules:
  0.0 210.1 jit_solution(867711834112606244)
XLA Ops:
  7.2 0.0 copy-start
  7.2 0.0 reduce-scatter.2.cloned.1.call-start
  7.2 0.7 compare_and_fusion
  8.0 6.5 %gather_fusion = bf16[256,512]{1,0:T(8,128)(2,1)S(1)} fusion(bf16[10240,512]{1,0:T(8,128)(2,1)} %bitcast.36, s32[1024]{0:T(1024)S(1)} %pad_clamp_fusion), kind=kCustom, calls=%fused_computation | custom fusion | bytes 525312 | tf_op jit(solution)/shard_map/jit(_take)/gather | solution.py:22
  14.5 0.1 convert_select_fusion
  14.7 47.2 %all-reduce.1 = bf16[256,512]{1,0:T(8,128)(2,1)S(1)} all-reduce(f32[256,512]{1,0:T(8,128)S(1)} %convert_select_fusion), channel_id=1, replica_groups=mesh['rows'=8,'grp'=4] {'rows','grp'}, use_global_device_ids=true, to_apply=%region_0.1 | all-reduce | flops 131072 | bytes 786432 | tf_op jit(solution)/shard_map/psum | solution.py:24
  61.9 9.6 %convolution_convert_fusion = bf16[10240,256]{1,0:T(8,128)(2,1)} fusion(bf16[10240,512]{1,0:T(8,128)(2,1)} %bitcast.37, bf16[10240,256]{1,0:T(8,128)(2,1)} %bitcast.38, bf16[256,512]{1,0:T(8,128)(2,1)S(1)} %all-reduce.1, bf16[256,256]{1,0:T(8,128)(2,1)} %param.9, s32[256]{0:T(256)S(1)} %iota_add_fusion), kind=kOutput, calls=%fused_computation.5 | convolution fusion | flops 4037148672 | bytes 21365760 | tf_op jit(solution)/shard_map/dot_general | solution.py:29
  71.5 10.4 %fusion.4 = f32[1024,4,256]{0,2,1:T(8,128)} fusion(bf16[4,2560,256]{2,1,0:T(8,128)(2,1)} %bitcast.39, bf16[2560,1024]{1,0:T(8,128)(2,1)} %param.10), kind=kOutput, calls=%fused_computation.8 | convolution fusion | flops 5368709120 | bytes 14680064 | tf_op jit(solution)/shard_map/nj,mnp->jmp/dot_general | solution.py:34
  81.9 0.0 reduce-scatter.2.cloned.1.call-update
  81.9 75.4 %reduce-scatter.2.cloned.1.call-done = f32[256,4,256]{0,2,1:T(8,128)} async-done(((f32[1024,4,256]{0,2,1:T(8,128)}), f32[256,4,256]{0,2,1:T(8,128)}) %reduce-scatter.2.cloned.1.call-update) | async-done | bytes 1048592 | tf_op jit(solution)/shard_map/reduce_scatter | solution.py:33
  157.3 1.3 convert_element_type.33
  158.6 0.4 copy.12
  159.0 13.2 %all_to_all.18 = bf16[256,4,256]{0,1,2:T(4,128)(2,1)S(1)} all-to-all(bf16[256,4,256]{0,1,2:T(4,128)(2,1)S(1)} %copy.12), channel_id=1, replica_groups=mesh['rows'=8,'grp'=4] {'rows'}, dimensions={2} | all-to-all | bytes 1048576 | tf_op jit(solution)/shard_map/all_to_all | solution.py:42
  172.2 0.3 copy.17
  172.5 0.1 all_to_all.16
  172.6 0.0 copy-done
  172.6 8.1 %convert_bitcast_fusion = bf16[32,1024,256]{1,2,0:T(8,128)(2,1)} fusion(bf16[256,32,32]{0,1,2:T(8,128)(2,1)S(1)} %all_to_all.16, bf16[32,1024]{1,0:T(8,128)(2,1)S(1)} %copy-done), kind=kOutput, calls=%fused_computation.1 | convolution fusion | flops 545259520 | bytes 17367040 | tf_op jit(solution)/shard_map/mi,jmp->pij/dot_general | solution.py:39
  180.8 0.0 copy-start.1
  180.8 22.5 %copy.14 = bf16[32,1024,256]{2,1,0:T(8,128)(2,1)} copy(bf16[32,1024,256]{1,2,0:T(8,128)(2,1)} %convert_bitcast_fusion) | data formatting | bytes 33554432
  203.2 0.0 copy-done.1
  (2 shorter events, 0.0 us)
Async XLA Ops:
  7.2 165.5 %copy-start = (bf16[32,1024]{1,0:T(8,128)(2,1)S(1)}, bf16[32,1024]{1,0:T(8,128)(2,1)}, u32[]{:S(2)}) copy-start(bf16[32,1024]{1,0:T(8,128)(2,1)} %param.11) | copy-start | bytes 196612
  7.2 150.1 %reduce-scatter.2.cloned.1.call-start = ((), (), s32[]{:S(2)}) async-start(), calls=%async_computation.2 | async-start | bytes 5242880 | tf_op jit(solution)/shard_map/reduce_scatter | solution.py:33
  180.8 22.5 %copy-start.1 = (bf16[32,1024]{1,0:T(8,128)(2,1)S(1)}, bf16[32,1024]{1,0:T(8,128)(2,1)}, u32[]{:S(2)}) copy-start(bf16[32,1024]{1,0:T(8,128)(2,1)} %param.11) | copy-start | bytes 196612
Sparse Core Ops, SparseCore 0:
  82.0 75.2 reduce-scatter.1
where the time goes:
time: 211 us; the launch traced here: 210 us
  waiting for transfers between devices  75.4 us (36%)
  blocking collectives  60.4 us (29%)
  local copies, waits for them, and re-layouts  29.8 us (14%)
  matrix products  28.1 us (13%)
  between operations  14.1 us (7%)
  other arithmetic  2.13 us (1%)
    reduce_scatter x1, waiting for transfers between devices, per_device(): lax.psum_scatter(jnp.einsum('nj,mnp->jmp', orbitals, new_vectors, preferr...  75.4 us
    psum x1, blocking collectives, per_device(): pivot_rows = lax.psum(picked, ('rows', 'grp')).astype(jnp.bfloat16)  47.2 us
    unnamed x5, local copies, waits for them, and re-layouts  22.5 us
    all_to_all x1, blocking collectives, per_device(): lax.all_to_all(half, 'rows', split_axis=2, concat_axis=1, tiled=True)  13.2 us
    dot_general x1, matrix products, per_device(): jnp.einsum('nj,mnp->jmp', orbitals, new_vectors, preferred_element_type=j...  10.4 us
    dot_general x1, matrix products, per_device(): jnp.dot(residual_columns, upper, preferred_element_type=jnp.float32)  9.58 us
    dot_general x1, matrix products, per_device(): jnp.einsum('mi,jmp->pij', slab_orbitals, lax.all_to_all(half, 'rows', spl...  8.14 us
    gather x1, local copies, waits for them, and re-layouts, per_device(): jnp.take(flat_prev, local_row, axis=0).astype(jnp.float32)  6.54 us
  transfers between devices with their start and end apart: 1, of which 1 were waited for; matrix products, arithmetic and copies ran while one was open for 0% of the time, Pallas kernels for 0%

commit v1 on v0

v1 whole, which is shorter than its diff:
```python
import functools

import jax
import jax.numpy as jnp
from jax import lax
from jax.experimental import pallas as pl
from jax.experimental.pallas import tpu as pltpu
from jax.sharding import PartitionSpec as P

F32 = jnp.float32
BF16 = jnp.bfloat16
MESH = pl.DeviceIdType.MESH


def exchange_kernel(R, G, x_ref, o_ref, buf_a, buf_b, buf_c, send_a, recv_a, send_b, recv_b, send_c, recv_c):
    r = lax.axis_index("rows")
    g = lax.axis_index("grp")
    row_peers = [(d, lax.rem(r + d, R)) for d in range(1, R)]
    grp_peers = [(d, lax.rem(g + d, G)) for d in range(1, G)]
    barrier = pltpu.get_barrier_semaphore()
    for _, peer in row_peers:
        pl.semaphore_signal(barrier, inc=1, device_id={"rows": peer, "grp": g}, device_id_type=MESH)
    for _, peer in grp_peers:
        pl.semaphore_signal(barrier, inc=1, device_id={"rows": r, "grp": peer}, device_id_type=MESH)
    pl.semaphore_wait(barrier, R - 1 + G - 1)

    def remote(src, dst, send, recv, device):
        return pltpu.make_async_remote_copy(
            src_ref=src, dst_ref=dst, send_sem=send, recv_sem=recv, device_id={"rows": device[0], "grp": device[1]}, device_id_type=MESH
        )

    first = [remote(x_ref.at[p], buf_a.at[d], send_a.at[d], recv_a.at[d], (p, g)) for d, p in row_peers]
    for copy in first:
        copy.start()
    total = x_ref[r].astype(F32)
    for (d, _), copy in zip(row_peers, first):
        copy.wait_recv()
        total = total + buf_a[d].astype(F32)
    buf_b[0] = total.astype(BF16)
    second = [remote(buf_b.at[0], buf_b.at[d], send_b.at[d], recv_b.at[d], (r, p)) for d, p in grp_peers]
    for copy in second:
        copy.start()
    for (d, _), copy in zip(grp_peers, second):
        copy.wait_recv()
        total = total + buf_b[d].astype(F32)
    buf_c[r] = total.astype(BF16)
    third = [remote(buf_c.at[r], buf_c.at[r], send_c.at[d], recv_c.at[d], (p, g)) for d, p in row_peers]
    for copy in third:
        copy.start()
    for copy in third:
        copy.wait_recv()
    for copy in first + second + third:
        copy.wait_send()
    o_ref[...] = buf_c[...]


def exchange(x, R, G):
    vmem = pl.BlockSpec(memory_space=pltpu.VMEM)
    _, c, k = x.shape
    dma = pltpu.SemaphoreType.DMA
    return pl.pallas_call(
        functools.partial(exchange_kernel, R, G),
        out_shape=jax.ShapeDtypeStruct(x.shape, BF16),
        in_specs=[vmem],
        out_specs=vmem,
        scratch_shapes=[
            pltpu.VMEM((R, c, k), BF16),
            pltpu.VMEM((G, c, k), BF16),
            pltpu.VMEM((R, c, k), BF16),
            dma((R,)), dma((R,)), dma((G,)), dma((G,)), dma((R,)), dma((R,)),
        ],
        compiler_params=pltpu.CompilerParams(collective_id=0, has_side_effects=True),
        name="pivot_exchange",
    )(x)


def vectors_kernel(pc_ref, prev_ref, rows_ref, inv_ref, out_ref):
    correction = lax.dot_general(
        prev_ref[...], rows_ref[...], (((1,), (1,)), ((), ())), preferred_element_type=F32
    )
    residual = (pc_ref[...].astype(F32) - correction).astype(BF16)
    shape = inv_ref.shape
    keep = lax.broadcasted_iota(jnp.int32, shape, 0) <= lax.broadcasted_iota(jnp.int32, shape, 1)
    upper = jnp.where(keep, inv_ref[...].astype(F32), 0.0).astype(BF16)
    out_ref[...] = jnp.dot(residual, upper, preferred_element_type=F32).astype(BF16)


def vectors(columns, prev, rows, inverse):
    m, p = columns.shape
    k = prev.shape[1]
    tile = 1024
    while m % tile:
        tile //= 2
    return pl.pallas_call(
        vectors_kernel,
        grid=(m // tile,),
        out_shape=jax.ShapeDtypeStruct((m, p), BF16),
        in_specs=[
            pl.BlockSpec((tile, p), lambda i: (i, 0)),
            pl.BlockSpec((tile, k), lambda i: (i, 0)),
            pl.BlockSpec((p, k), lambda i: (0, 0)),
            pl.BlockSpec((p, p), lambda i: (0, 0)),
        ],
        out_specs=pl.BlockSpec((tile, p), lambda i: (i, 0)),
        name="new_vectors",
    )(columns, prev, rows, inverse)


def half_kernel(R, G, new_hbm, orb_hbm, out_hbm, new_v, orb_v, turned, send, in_sem, own_sem, send_sem, recv_sem):
    r = lax.axis_index("rows")
    g = lax.axis_index("grp")
    N = R * G
    mu_dev, nu, p = new_v.shape
    _, _, _, pl_dev, j_dev = send.shape

    def load(mu):
        return pltpu.make_async_copy(new_hbm.at[mu], new_v.at[mu], in_sem.at[mu])

    load_orb = pltpu.make_async_copy(orb_hbm, orb_v, in_sem.at[mu_dev])
    load(0).start()
    load_orb.start()
    for mu in range(1, mu_dev):
        load(mu).start()

    barrier = pltpu.get_barrier_semaphore()
    me = r * G + g

    @pl.loop(1, N)
    def _(d):
        peer = lax.rem(me + d, N)
        pl.semaphore_signal(
            barrier, inc=1, device_id={"rows": peer // G, "grp": lax.rem(peer, G)}, device_id_type=MESH
        )

    chunk = 256
    shape = (p, p)
    eye = jnp.where(
        lax.broadcasted_iota(jnp.int32, shape, 0) == lax.broadcasted_iota(jnp.int32, shape, 1), 1.0, 0.0
    ).astype(BF16)

    def turn(mu):
        @pl.loop(0, nu // chunk)
        def _(i):
            at = pl.ds(pl.multiple_of(i * chunk, chunk), chunk)
            turned[:, at] = lax.dot_general(
                eye, new_v[mu, at, :], (((1,), (1,)), ((), ())), preferred_element_type=F32
            ).astype(BF16)

    pl.semaphore_wait(barrier, N - 1)
    load_orb.wait()

    @pl.loop(0, mu_dev)
    def _(mu):
        load(mu).wait()
        turn(mu)
        slot = (g * R + r) * mu_dev + mu

        @pl.loop(0, G)
        def _(d):
            to = lax.rem(g + 1 + d, G)
            cols = pl.ds(pl.multiple_of(to * j_dev, j_dev), j_dev)
            block = jnp.dot(turned[...], orb_v[:, cols], preferred_element_type=F32)
            for k in range(R):
                send[mu, to, k] = block[k * pl_dev : (k + 1) * pl_dev].astype(BF16)

            for k in range(R):
                peer = lax.rem(r + k, R)
                src = send.at[mu, to, peer]
                dst = out_hbm.at[slot]

                def away():
                    pltpu.make_async_remote_copy(
                        src_ref=src, dst_ref=dst, send_sem=send_sem, recv_sem=recv_sem,
                        device_id={"rows": peer, "grp": to}, device_id_type=MESH,
                    ).start()

                if k:
                    away()
                else:
                    pl.when(to != g)(away)

                    @pl.when(to == g)
                    def _():
                        pltpu.make_async_copy(src, dst, own_sem).start()

    others = out_hbm.at[pl.ds(0, (N - 1) * mu_dev)]
    own = out_hbm.at[pl.ds(0, mu_dev)]
    pltpu.make_async_copy(own, own, own_sem).wait()
    pltpu.make_async_copy(others, others, send_sem).wait()
    pltpu.make_async_copy(others, others, recv_sem).wait()


def half_partials(new, orbitals, R, G):
    mu_dev, nu, p = new.shape
    nj = orbitals.shape[1]
    hbm = pl.BlockSpec(memory_space=pl.ANY)
    dma = pltpu.SemaphoreType.DMA
    return pl.pallas_call(
        functools.partial(half_kernel, R, G),
        out_shape=jax.ShapeDtypeStruct((R * G * mu_dev, p // R, nj // G), BF16),
        in_specs=[hbm, hbm],
        out_specs=hbm,
        scratch_shapes=[
            pltpu.VMEM((mu_dev, nu, p), BF16),
            pltpu.VMEM((nu, nj), BF16),
            pltpu.VMEM((p, nu), BF16),
            pltpu.VMEM((mu_dev, G, R, p // R, nj // G), BF16),
            dma((mu_dev + 1,)), dma(()), dma(()), dma(()),
        ],
        compiler_params=pltpu.CompilerParams(collective_id=1, has_side_effects=True),
        name="half_exchange",
    )(new, orbitals)


def block_kernel(part_ref, slab_ref, out_ref, half_ref, sorted_ref, slab_t_ref):
    groups, rows, _ = part_ref.shape
    mus = slab_ref.shape[0]
    block = out_ref.shape[0]
    vecs = rows // mus
    step = pl.program_id(0)

    @pl.when(step == 0)
    def _():
        slab_t_ref[...] = slab_ref[...].astype(F32).T.astype(BF16)
        piece = 128

        @pl.loop(0, rows // piece)
        def _(i):
            at = pl.ds(pl.multiple_of(i * piece, piece), piece)
            total = part_ref[0, at, :].astype(F32)
            for k in range(1, groups):
                total = total + part_ref[k, at, :].astype(F32)
            half_ref[at, :] = total.astype(BF16)

        shift = mus.bit_length() - 1

        @pl.loop(0, rows // piece)
        def _(i):
            at = pl.ds(pl.multiple_of(i * piece, piece), piece)
            row = lax.broadcasted_iota(jnp.int32, (piece, rows), 0) + i * piece
            col = lax.broadcasted_iota(jnp.int32, (piece, rows), 1)
            source = (row & (mus - 1)) * vecs + lax.shift_right_logical(row, shift)
            pick = jnp.where(source == col, 1.0, 0.0).astype(BF16)
            sorted_ref[at, :] = jnp.dot(pick, half_ref[...], preferred_element_type=F32).astype(BF16)

    for q in range(block):
        at = pl.ds(pl.multiple_of((step * block + q) * mus, mus), mus)
        out_ref[q] = jnp.dot(slab_t_ref[...], sorted_ref[at, :], preferred_element_type=F32).astype(BF16)


def orbital_block(parts, slab):
    groups, rows, j = parts.shape
    mus, i = slab.shape
    assert mus & (mus - 1) == 0
    vecs = rows // mus
    block = 4 if vecs % 4 == 0 else 1
    return pl.pallas_call(
        block_kernel,
        grid=(vecs // block,),
        out_shape=jax.ShapeDtypeStruct((vecs, i, j), BF16),
        in_specs=[
            pl.BlockSpec((groups, rows, j), lambda s: (0, 0, 0)),
            pl.BlockSpec((mus, i), lambda s: (0, 0)),
        ],
        out_specs=pl.BlockSpec((block, i, j), lambda s: (s, 0, 0)),
        scratch_shapes=[
            pltpu.VMEM((rows, j), BF16),
            pltpu.VMEM((rows, j), BF16),
            pltpu.VMEM((i, mus), BF16),
        ],
        name="orbital_block",
    )(parts, slab)


def per_device(R, G, pivot_columns, previous, pivots, pivot_inverse, orbitals, slab_orbitals):
    mu_dev, nu_dev, prev_count = previous.shape
    count = pivot_columns.shape[2]
    nbas = nu_dev * G
    row_index = lax.axis_index("rows")
    grp_index = lax.axis_index("grp")
    first_local = pivots // nbas - row_index * mu_dev
    second_local = pivots % nbas - grp_index * nu_dev
    owned = (
        (first_local >= 0) & (first_local < mu_dev) & (second_local >= 0) & (second_local < nu_dev)
    )
    local_row = jnp.where(owned, first_local * nu_dev + second_local, 0)
    flat_prev = previous.reshape(mu_dev * nu_dev, prev_count)
    picked = jnp.where(
        owned[:, None], flat_prev.at[local_row].get(mode="promise_in_bounds"), jnp.zeros((), BF16)
    )
    pivot_rows = exchange(picked.reshape(R, count // R, prev_count), R, G).reshape(count, prev_count)
    new_flat = vectors(pivot_columns.reshape(-1, count), flat_prev, pivot_rows, pivot_inverse)
    new_vectors = new_flat.reshape(mu_dev, nu_dev, count)
    parts = half_partials(new_vectors, orbitals, R, G)
    parts = parts.reshape(G, R * mu_dev * (count // R), orbitals.shape[1] // G)
    return new_vectors, orbital_block(parts, slab_orbitals)


def solution(mesh):
    R, G = mesh.shape["rows"], mesh.shape["grp"]
    in_specs = (P("rows", "grp", None), P("rows", "grp", None), P(), P(), P("grp", None), P())
    out_specs = (P("rows", "grp", None), P("rows", None, "grp"))
    return jax.shard_map(
        functools.partial(per_device, R, G), mesh=mesh, in_specs=in_specs, out_specs=out_specs,
        check_vma=False,
    )
```

time: 211 us -> 108 us (0.51)
  Pallas kernels: 0 us -> 98.4 us
  waiting for transfers between devices: 75.4 us -> 0 us
  blocking collectives: 60.4 us -> 0 us
  matrix products: 28.1 us -> 0 us
  local copies, waits for them, and re-layouts: 29.8 us -> 6.62 us
  between operations: 14.1 us -> 0.66 us
    pallas_call x0 -> x4, Pallas kernels: none -> 98.4 us  [the longest x1 52.2 us: half_partials(): pl.pallas_call(functools.partial(half_kernel, R, G), out_shape=jax.ShapeD...]
    reduce_scatter x1 -> x0, waiting for transfers between devices: 75.4 us -> none  [per_device(): lax.psum_scatter(jnp.einsum('nj,mnp->jmp', orbitals, new_vectors, preferr...]
    psum x1 -> x0, blocking collectives: 47.2 us -> none  [per_device(): pivot_rows = lax.psum(picked, ('rows', 'grp')).astype(jnp.bfloat16)]
    dot_general x3 -> x0, matrix products: 28.1 us -> none  [the longest x1 10.4 us: per_device(): jnp.einsum('nj,mnp->jmp', orbitals, new_vectors, preferred_element_type=j...]
    unnamed x5 -> x0, local copies, waits for them, and re-layouts: 22.5 us -> none
    all_to_all x1 -> x0, blocking collectives: 13.2 us -> none  [per_device(): lax.all_to_all(half, 'rows', split_axis=2, concat_axis=1, tiled=True)]
  transfers between devices with their start and end apart: 1 -> 0, of which waited for: 1 -> 0; matrix products, arithmetic and copies ran while one was open for 0% -> 0% of each run, Pallas kernels for 0% -> 0%
where the time goes in v1:
time: 108 us; the launch traced here: 107 us
  Pallas kernels  98.4 us (91%)
  local copies, waits for them, and re-layouts  6.62 us (6%)
  other arithmetic  1.51 us (1%)
    pallas_call x1, Pallas kernels, half_partials(): pl.pallas_call(functools.partial(half_kernel, R, G), out_shape=jax.ShapeD...  52.2 us
    pallas_call x1, Pallas kernels, exchange(): pl.pallas_call(functools.partial(exchange_kernel, R, G), out_shape=jax.Sh...  20.1 us
    pallas_call x1, Pallas kernels, vectors(): pl.pallas_call(vectors_kernel, grid=(m // tile,), out_shape=jax.ShapeDtyp...  13.5 us
    pallas_call x1, Pallas kernels, orbital_block(): pl.pallas_call(block_kernel, grid=(vecs // block,), out_shape=jax.ShapeDt...  12.7 us
    gather x1, local copies, waits for them, and re-layouts, per_device(): flat_prev.at[local_row].get(mode='promise_in_bounds')  6.54 us

profile of v1, /device:TPU:0, one launch (start us, length us, event | category | flops | bytes accessed | tf_op | source)
XLA Modules:
  0.0 107.2 jit_solution(5466091038501690274)
XLA Ops:
  0.6 0.7 compare_select_fusion
  1.3 0.1 broadcast_in_dim.20
  1.4 6.5 %gather_fusion = bf16[256,512]{1,0:T(8,128)(2,1)S(1)} fusion(bf16[10240,512]{1,0:T(8,128)(2,1)} %bitcast.8, s32[1024]{0:T(1024)S(1)} %pad_clamp_fusion), kind=kCustom, calls=%fused_computation | custom fusion | bytes 525312 | tf_op jit(solution)/shard_map/gather | solution.py:289
  8.0 0.8 broadcast_select_fusion.x_ref
  8.8 20.1 %pivot_exchange.1 = bf16[8,32,512]{2,1,0:T(8,128)(2,1)} custom-call(bf16[8,32,512]{2,1,0:T(8,128)(2,1)} %broadcast_select_fusion.x_ref), custom_call_target="tpu_custom_call" | custom-call | tf_op jit(solution)/shard_map/pivot_exchange/pallas_call | solution.py:61
  28.9 13.5 %new_vectors.1 = bf16[10240,256]{1,0:T(8,128)(2,1)} custom-call(bf16[10240,256]{1,0:T(8,128)(2,1)} %bitcast.11, bf16[10240,512]{1,0:T(8,128)(2,1)} %bitcast.9, bf16[256,512]{1,0:T(8,128)(2,1)} %bitcast.13, bf16[256,256]{1,0:T(8,128)(2,1)} %inv_ref.1), custom_call_target="tpu_custom_call" | custom-call | tf_op jit(solution)/shard_map/new_vectors/pallas_call | solution.py:94
  42.4 52.2 %half_exchange.1 = bf16[128,32,256]{2,1,0:T(8,128)(2,1)} custom-call(bf16[4,2560,256]{2,1,0:T(8,128)(2,1)} %bitcast.6, bf16[2560,1024]{1,0:T(8,128)(2,1)} %orb_hbm.1), custom_call_target="tpu_custom_call" | custom-call | tf_op jit(solution)/shard_map/half_exchange/pallas_call | solution.py:198
  94.5 12.7 %orbital_block.1 = bf16[32,1024,256]{2,1,0:T(8,128)(2,1)} custom-call(bf16[4,1024,256]{2,1,0:T(8,128)(2,1)} %bitcast.10, bf16[32,1024]{1,0:T(8,128)(2,1)} %slab_ref.1), custom_call_target="tpu_custom_call" | custom-call | tf_op jit(solution)/shard_map/orbital_block/pallas_call | solution.py:257
  (1 shorter events, 0.0 us)

commit v2 on v0

v2 whole, which is shorter than its diff:
```python
import functools

import jax
import jax.numpy as jnp
from jax import lax
from jax.experimental import pallas as pl
from jax.experimental.pallas import tpu as pltpu
from jax.sharding import PartitionSpec as P

F32 = jnp.float32
BF16 = jnp.bfloat16
MESH = pl.DeviceIdType.MESH


def relayed(G):
    return G >= 4


def fused_kernel(
    R, G, x_ref, pc_hbm, prev_hbm, inv_ref, orb_hbm, out_hbm, new_hbm,
    buf_a, buf_b, buf_c, rows_wide, rows_v, upper_v, new_v, prev_v, orb_v, turned, block_v, send, relay,
    send_a, recv_a, send_b, recv_b, send_c, recv_c, in_sem, new_sem, own_sem, send_sem, recv_sem, relay_sem,
):
    r = lax.axis_index("rows")
    g = lax.axis_index("grp")
    N = R * G
    me = r * G + g
    mu_dev, nu, p = new_v.shape
    _, _, _, pl_dev, j_dev = send.shape
    c = buf_c.shape[1]

    def load(mu):
        return (
            pltpu.make_async_copy(prev_hbm.at[mu], prev_v.at[mu], in_sem.at[2 * mu]),
            pltpu.make_async_copy(pc_hbm.at[mu], new_v.at[mu], in_sem.at[2 * mu + 1]),
        )

    load_orb = pltpu.make_async_copy(orb_hbm, orb_v, in_sem.at[2 * mu_dev])
    for mu in range(mu_dev):
        for copy in load(mu):
            copy.start()
        if mu == 0:
            load_orb.start()

    barrier = pltpu.get_barrier_semaphore()

    @pl.loop(1, N)
    def _(d):
        peer = lax.rem(me + d, N)
        pl.semaphore_signal(
            barrier, inc=1, device_id={"rows": peer // G, "grp": lax.rem(peer, G)}, device_id_type=MESH
        )

    shape = (p, p)
    low = lax.broadcasted_iota(jnp.int32, shape, 0)
    high = lax.broadcasted_iota(jnp.int32, shape, 1)
    upper_v[...] = jnp.where(low <= high, inv_ref[...].astype(F32), 0.0).astype(BF16)
    pl.semaphore_wait(barrier, N - 1)

    def remote(src, dst, send, recv, row, grp):
        return pltpu.make_async_remote_copy(
            src_ref=src, dst_ref=dst, send_sem=send, recv_sem=recv,
            device_id={"rows": row, "grp": grp}, device_id_type=MESH,
        )

    row_peers = [(d, lax.rem(r + d, R)) for d in range(1, R)]
    grp_peers = [(d, lax.rem(g + d, G)) for d in range(1, G)]
    first = [remote(x_ref.at[q], buf_a.at[d], send_a.at[d], recv_a.at[d], q, g) for d, q in row_peers]
    for copy in first:
        copy.start()
    total = x_ref[r].astype(F32)
    for (d, _), copy in zip(row_peers, first):
        copy.wait_recv()
        total = total + buf_a[d].astype(F32)
    buf_b[0] = total.astype(BF16)
    second = [remote(buf_b.at[0], buf_b.at[d], send_b.at[d], recv_b.at[d], r, q) for d, q in grp_peers]
    for copy in second:
        copy.start()
    for (d, _), copy in zip(grp_peers, second):
        copy.wait_recv()
        total = total + buf_b[d].astype(F32)
    buf_c[r] = total.astype(BF16)
    third = [remote(buf_c.at[r], buf_c.at[r], send_c.at[d], recv_c.at[d], q, g) for d, q in row_peers]
    for copy in third:
        copy.start()
    for copy in third:
        copy.wait_recv()
    for copy in first + second + third:
        copy.wait_send()
    for k in range(R):
        rows_wide[k * c : (k + 1) * c, :] = buf_c[k].astype(F32)
    rows_v[...] = rows_wide[...].astype(BF16)
    load_orb.wait()

    chunk = 512 if nu % 512 == 0 else 256
    edge = (g == 0) | (g == G - 1)
    across = G - 1 - g
    falling = (g == 0) | ((2 * g >= G) & (g != G - 1))

    def store_new(mu):
        return pltpu.make_async_copy(new_v.at[mu], new_hbm.at[mu], new_sem.at[mu])

    @pl.loop(0, mu_dev)
    def _(mu):
        for copy in load(mu):
            copy.wait()
        eye = jnp.where(
            lax.broadcasted_iota(jnp.int32, shape, 0) == lax.broadcasted_iota(jnp.int32, shape, 1), 1.0, 0.0
        ).astype(BF16)

        @pl.loop(0, nu // chunk)
        def _(i):
            at = pl.ds(pl.multiple_of(i * chunk, chunk), chunk)
            correction = lax.dot_general(
                prev_v[mu, at, :], rows_v[...], (((1,), (1,)), ((), ())), preferred_element_type=F32
            )
            residual = (new_v[mu, at, :].astype(F32) - correction).astype(BF16)
            made = jnp.dot(residual, upper_v[...], preferred_element_type=F32).astype(BF16)
            new_v[mu, at, :] = made
            turned[:, at] = lax.dot_general(
                eye, made, (((1,), (1,)), ((), ())), preferred_element_type=F32
            ).astype(BF16)

        store_new(mu).start()
        slot = (g * R + r) * mu_dev + mu

        @pl.loop(0, G)
        def _(d):
            to = jnp.where(falling, G - 1 - d, d)
            cols = pl.ds(pl.multiple_of(to * j_dev, j_dev), j_dev)
            block_v[...] = jnp.dot(turned[...], orb_v[:, cols], preferred_element_type=F32)

            def deliver():
                for k in range(R):
                    peer = lax.rem(r + k, R)
                    src = send.at[mu, to, peer]
                    dst = out_hbm.at[slot]

                    def away():
                        remote(src, dst, send_sem, recv_sem, peer, to).start()

                    if k:
                        away()
                    else:
                        pl.when(to != g)(away)

                        @pl.when(to == g)
                        def _():
                            pltpu.make_async_copy(src, dst, own_sem).start()

            def keep():
                for k in range(R):
                    send[mu, to, k] = block_v[k * pl_dev : (k + 1) * pl_dev, :].astype(BF16)

            if not relayed(G):
                keep()
                deliver()
                return
            adds = ((g == 1) & (to == G - 1)) | ((g == G - 2) & (to == 0))
            hands = edge & (to == across)

            @pl.when(adds)
            def _():
                pltpu.make_async_copy(relay.at[mu], relay.at[mu], relay_sem.at[mu]).wait()
                for k in range(R):
                    mine = block_v[k * pl_dev : (k + 1) * pl_dev, :]
                    send[mu, to, k] = (mine + relay[mu, k].astype(F32)).astype(BF16)

            pl.when(jnp.logical_not(adds))(keep)

            @pl.when(hands)
            def _():
                via = jnp.where(g == 0, 1, G - 2)
                remote(send.at[mu, to], relay.at[mu], send_sem, relay_sem.at[mu], r, via).start()

            pl.when(jnp.logical_not(hands))(deliver)

    own = out_hbm.at[pl.ds(0, mu_dev)]
    pltpu.make_async_copy(own, own, own_sem).wait()
    for mu in range(mu_dev):
        store_new(mu).wait()
    every = out_hbm.at[pl.ds(0, (N - 1) * mu_dev)]
    pltpu.make_async_copy(every, every, send_sem).wait()
    if relayed(G):
        @pl.when(edge)
        def _():
            fewer = out_hbm.at[pl.ds(0, (N - R - 1) * mu_dev)]
            pltpu.make_async_copy(fewer, fewer, recv_sem).wait()

        @pl.when(jnp.logical_not(edge))
        def _():
            pltpu.make_async_copy(every, every, recv_sem).wait()
    else:
        pltpu.make_async_copy(every, every, recv_sem).wait()


def fused(picked, columns, previous, inverse, orbitals, R, G):
    mu_dev, nu, p = columns.shape
    k = previous.shape[2]
    c = p // R
    nj = orbitals.shape[1]
    hbm = pl.BlockSpec(memory_space=pl.ANY)
    vmem = pl.BlockSpec(memory_space=pltpu.VMEM)
    dma = pltpu.SemaphoreType.DMA
    return pl.pallas_call(
        functools.partial(fused_kernel, R, G),
        out_shape=(
            jax.ShapeDtypeStruct((R * G * mu_dev, c, nj // G), BF16),
            jax.ShapeDtypeStruct(columns.shape, BF16),
        ),
        in_specs=[vmem, hbm, hbm, vmem, hbm],
        out_specs=(hbm, hbm),
        scratch_shapes=[
            pltpu.VMEM((R, c, k), BF16),
            pltpu.VMEM((G, c, k), BF16),
            pltpu.VMEM((R, c, k), BF16),
            pltpu.VMEM((p, k), F32),
            pltpu.VMEM((p, k), BF16),
            pltpu.VMEM((p, p), BF16),
            pltpu.VMEM((mu_dev, nu, p), BF16),
            pltpu.VMEM((mu_dev, nu, k), BF16),
            pltpu.VMEM((nu, nj), BF16),
            pltpu.VMEM((p, nu), BF16),
            pltpu.VMEM((p, nj // G), F32),
            pltpu.VMEM((mu_dev, G, R, c, nj // G), BF16),
            pltpu.VMEM((mu_dev, R, c, nj // G), BF16),
            dma((R,)), dma((R,)), dma((G,)), dma((G,)), dma((R,)), dma((R,)),
            dma((2 * mu_dev + 1,)), dma((mu_dev,)), dma(()), dma(()), dma(()), dma((mu_dev,)),
        ],
        compiler_params=pltpu.CompilerParams(
            collective_id=0, has_side_effects=True, vmem_limit_bytes=60 * 1024 * 1024
        ),
        name="fused_exchange",
    )(picked, columns, previous, inverse, orbitals)


def block_kernel(part_ref, slab_ref, out_ref, half_ref, sorted_ref, slab_t_ref):
    groups, rows, _ = part_ref.shape
    mus = slab_ref.shape[0]
    block = out_ref.shape[0]
    vecs = rows // mus
    step = pl.program_id(0)
    g = lax.axis_index("grp")

    @pl.when(step == 0)
    def _():
        slab_t_ref[...] = slab_ref[...].astype(F32).T.astype(BF16)
        piece = 128

        @pl.loop(0, rows // piece)
        def _(i):
            at = pl.ds(pl.multiple_of(i * piece, piece), piece)
            total = jnp.zeros((piece, part_ref.shape[2]), F32)
            for k in range(groups):
                part = part_ref[k, at, :].astype(F32)
                if relayed(groups) and k in (0, groups - 1):
                    part = jnp.where(g == groups - 1 - k, 0.0, part)
                total = total + part
            half_ref[at, :] = total.astype(BF16)

        shift = mus.bit_length() - 1

        @pl.loop(0, rows // piece)
        def _(i):
            at = pl.ds(pl.multiple_of(i * piece, piece), piece)
            row = lax.broadcasted_iota(jnp.int32, (piece, rows), 0) + i * piece
            col = lax.broadcasted_iota(jnp.int32, (piece, rows), 1)
            source = (row & (mus - 1)) * vecs + lax.shift_right_logical(row, shift)
            pick = jnp.where(source == col, 1.0, 0.0).astype(BF16)
            sorted_ref[at, :] = jnp.dot(pick, half_ref[...], preferred_element_type=F32).astype(BF16)

    for q in range(block):
        at = pl.ds(pl.multiple_of((step * block + q) * mus, mus), mus)
        out_ref[q] = jnp.dot(slab_t_ref[...], sorted_ref[at, :], preferred_element_type=F32).astype(BF16)


def orbital_block(parts, slab):
    groups, rows, j = parts.shape
    mus, i = slab.shape
    assert mus & (mus - 1) == 0
    vecs = rows // mus
    block = 4 if vecs % 4 == 0 else 1
    return pl.pallas_call(
        block_kernel,
        grid=(vecs // block,),
        out_shape=jax.ShapeDtypeStruct((vecs, i, j), BF16),
        in_specs=[
            pl.BlockSpec((groups, rows, j), lambda s: (0, 0, 0)),
            pl.BlockSpec((mus, i), lambda s: (0, 0)),
        ],
        out_specs=pl.BlockSpec((block, i, j), lambda s: (s, 0, 0)),
        scratch_shapes=[
            pltpu.VMEM((rows, j), BF16),
            pltpu.VMEM((rows, j), BF16),
            pltpu.VMEM((i, mus), BF16),
        ],
        name="orbital_block",
    )(parts, slab)


def per_device(R, G, pivot_columns, previous, pivots, pivot_inverse, orbitals, slab_orbitals):
    mu_dev, nu_dev, prev_count = previous.shape
    count = pivot_columns.shape[2]
    nbas = nu_dev * G
    row_index = lax.axis_index("rows")
    grp_index = lax.axis_index("grp")
    first_local = pivots // nbas - row_index * mu_dev
    second_local = pivots % nbas - grp_index * nu_dev
    owned = (
        (first_local >= 0) & (first_local < mu_dev) & (second_local >= 0) & (second_local < nu_dev)
    )
    local_row = jnp.where(owned, first_local * nu_dev + second_local, 0)
    flat_prev = previous.reshape(mu_dev * nu_dev, prev_count)
    picked = jnp.where(
        owned[:, None], flat_prev.at[local_row].get(mode="promise_in_bounds"), jnp.zeros((), BF16)
    )
    parts, new_vectors = fused(
        picked.reshape(R, count // R, prev_count), pivot_columns, previous, pivot_inverse, orbitals, R, G
    )
    parts = parts.reshape(G, R * mu_dev * (count // R), orbitals.shape[1] // G)
    return new_vectors, orbital_block(parts, slab_orbitals)


def solution(mesh):
    R, G = mesh.shape["rows"], mesh.shape["grp"]
    in_specs = (P("rows", "grp", None), P("rows", "grp", None), P(), P(), P("grp", None), P())
    out_specs = (P("rows", "grp", None), P("rows", None, "grp"))
    return jax.shard_map(
        functools.partial(per_device, R, G), mesh=mesh, in_specs=in_specs, out_specs=out_specs,
        check_vma=False,
    )
```

time: 211 us -> 91.9 us (0.44)
  Pallas kernels: 0 us -> 77.7 us
  waiting for transfers between devices: 75.4 us -> 0 us
  blocking collectives: 60.4 us -> 0 us
  matrix products: 28.1 us -> 0 us
  local copies, waits for them, and re-layouts: 29.8 us -> 11.8 us
  between operations: 14.1 us -> 0.65 us
    pallas_call x0 -> x2, Pallas kernels: none -> 77.7 us  [the longest x1 64.9 us: fused(): pl.pallas_call(functools.partial(fused_kernel, R, G), out_shape=(jax.Shap...]
    reduce_scatter x1 -> x0, waiting for transfers between devices: 75.4 us -> none  [per_device(): lax.psum_scatter(jnp.einsum('nj,mnp->jmp', orbitals, new_vectors, preferr...]
    psum x1 -> x0, blocking collectives: 47.2 us -> none  [per_device(): pivot_rows = lax.psum(picked, ('rows', 'grp')).astype(jnp.bfloat16)]
    dot_general x3 -> x0, matrix products: 28.1 us -> none  [the longest x1 10.4 us: per_device(): jnp.einsum('nj,mnp->jmp', orbitals, new_vectors, preferred_element_type=j...]
    unnamed x5 -> x1, local copies, waits for them, and re-layouts: 22.5 us -> 5.18 us
    all_to_all x1 -> x0, blocking collectives: 13.2 us -> none  [per_device(): lax.all_to_all(half, 'rows', split_axis=2, concat_axis=1, tiled=True)]
  transfers between devices with their start and end apart: 1 -> 0, of which waited for: 1 -> 0; matrix products, arithmetic and copies ran while one was open for 0% -> 0% of each run, Pallas kernels for 0% -> 0%
where the time goes in v2:
time: 91.9 us; the launch traced here: 91.6 us
  Pallas kernels  77.7 us (85%)
  local copies, waits for them, and re-layouts  11.8 us (13%)
  other arithmetic  1.51 us (2%)
    pallas_call x1, Pallas kernels, fused(): pl.pallas_call(functools.partial(fused_kernel, R, G), out_shape=(jax.Shap...  64.9 us
    pallas_call x1, Pallas kernels, orbital_block(): pl.pallas_call(block_kernel, grid=(vecs // block,), out_shape=jax.ShapeDt...  12.8 us
    gather x1, local copies, waits for them, and re-layouts, per_device(): flat_prev.at[local_row].get(mode='promise_in_bounds')  6.54 us
    unnamed x1, local copies, waits for them, and re-layouts  5.18 us

profile of v2, /device:TPU:0, one launch (start us, length us, event | category | flops | bytes accessed | tf_op | source)
XLA Modules:
  0.0 91.6 jit_solution(9356280429620039551)
XLA Ops:
  0.6 0.7 compare_select_fusion
  1.3 0.1 broadcast_in_dim.20
  1.4 6.5 %gather_fusion = bf16[256,512]{1,0:T(8,128)(2,1)S(1)} fusion(bf16[10240,512]{1,0:T(8,128)(2,1)} %bitcast.3, s32[1024]{0:T(1024)S(1)} %pad_clamp_fusion), kind=kCustom, calls=%fused_computation | custom fusion | bytes 525312 | tf_op jit(solution)/shard_map/gather | solution.py:315
  8.0 0.8 broadcast_select_fusion.x_ref
  8.8 64.9 %fused_exchange.1 = (bf16[128,32,256]{2,1,0:T(8,128)(2,1)}, bf16[4,2560,256]{2,1,0:T(8,128)(2,1)}) custom-call(bf16[8,32,512]{2,1,0:T(8,128)(2,1)} %broadcast_select_fusion.x_ref, bf16[4,2560,256]{2,1,0:T(8,128)(2,1)} %pc_hbm.1, bf16[4,2560,512]{2,1,0:T(8,128)(2,1)} %prev_hbm.1, bf16[256,256]{1,0:T(8,128)(2,1)} %inv_ref.1, bf16[2560,1024]{1,0:T(8,128)(2,1)} %orb_hbm.1), custom_call_target="tpu_custom_call" | custom-call | tf_op jit(solution)/shard_map/fused_exchange/pallas_call | solution.py:205
  73.7 12.8 %orbital_block.1 = bf16[32,1024,256]{2,1,0:T(8,128)(2,1)} custom-call(bf16[4,1024,256]{2,1,0:T(8,128)(2,1)} %bitcast.4, bf16[32,1024]{1,0:T(8,128)(2,1)} %slab_ref.1), custom_call_target="tpu_custom_call" | custom-call | tf_op jit(solution)/shard_map/orbital_block/pallas_call | solution.py:283
  86.5 5.2 %copy.9 = bf16[4,2560,256]{2,1,0:T(8,128)(2,1)} copy(bf16[4,2560,256]{2,1,0:T(8,128)(2,1)} %get-tuple-element.10) | data formatting | bytes 10485760
  (1 shorter events, 0.0 us)
